TPU v7x, 32 devices: a whole 2x2x4 slice. The times are simulated.
32 devices in a mesh: dp: 8 (over y, x, core), tensor: 4 (over z).
Axes of the slice: x: 2, y: 2, z: 4, core: 2. Of those that a mesh axis runs over, the one named last changes fastest.
Arguments:
- block_in: bfloat16 [12288, 1536], P(('dp', 'tensor')), may hold values from -6 to 6
- cotangent: bfloat16 [12288, 1536], P(('dp', 'tensor')), may hold values from -6 to 6
- segment_ids: int32 [24, 512], P('dp'), may hold values from 0 to 3, never falling along the last dimension, each value on 1 to 256 neighbouring positions
- attn_gain: bfloat16 [1536], P('dp'), may hold values from 0.5 to 1.5
- qkv_weight: bfloat16 [1536, 3072], P('dp', 'tensor'), may hold values from -4 to 4
- out_weight: bfloat16 [1536, 1536], P('tensor', 'dp'), may hold values from -1.25 to 1.25
- mlp_gain: bfloat16 [1536], P('dp'), may hold values from 0.5 to 1.5
- gate_weight: bfloat16 [1536, 4096], P('dp', 'tensor'), may hold values from -0.15625 to 0.15625
- up_weight: bfloat16 [1536, 4096], P('dp', 'tensor'), may hold values from -0.15625 to 0.15625
- down_weight: bfloat16 [4096, 1536], P('tensor', 'dp'), may hold values from -0.09375 to 0.09375
Outputs:
- block_out: bfloat16 [12288, 1536], P(('dp', 'tensor'))
- input_grad: bfloat16 [12288, 1536], P(('dp', 'tensor'))
- attn_gain_grad: float32 [1536], P('dp')
- qkv_grad: float32 [1536, 3072], P('dp', 'tensor')
- out_grad: float32 [1536, 1536], P('tensor', 'dp')
- mlp_gain_grad: float32 [1536], P('dp')
- gate_grad: float32 [1536, 4096], P('dp', 'tensor')
- up_grad: float32 [1536, 4096], P('dp', 'tensor')
- down_grad: float32 [4096, 1536], P('tensor', 'dp')
Inputs may be any that keep to these rules, and one draw needn't show every extreme that they name: `segment_ids`: segment numbers never fall along a sequence; a segment holds at most 256 tokens of its sequence, and some segment of every sequence holds exactly that many.
All inputs are finite; a program needn't handle non-finite values.
Results may differ from a plain program's by a relative error of at most 0.025.
The roundings to bfloat16 on the way count: a program that leaves them out, or rounds other values in their place, can miss the bound.
Values may be sent and summed in bfloat16 or wider, within the bound.
A program may use at most 192 MiB of HBM per device.

v0:
```python
import functools

import jax
import jax.numpy as jnp
import numpy as np
from jax import lax
from jax.experimental import pallas as pl
from jax.experimental.pallas import tpu as pltpu
from jax.sharding import PartitionSpec as P

QUERY_HEADS = 16
KEY_VALUE_HEADS = 8
HEAD_SIZE = 96


EPS = 1e-05
ROPE_BASE = 100000.0
NEG_FILL = -1e30


def doc_positions(segments):
    length = segments.shape[1]
    position_index = jnp.broadcast_to(jnp.arange(length, dtype=jnp.int32)[None, :], segments.shape)
    change = jnp.concatenate(
        [jnp.ones((segments.shape[0], 1), dtype=bool), segments[:, 1:] != segments[:, :-1]], axis=1
    )
    starts = lax.cummax(jnp.where(change, position_index, jnp.zeros_like(position_index)), axis=1)
    return position_index - starts


def rotary_tables(segments):
    half_dim = HEAD_SIZE // 2
    frequency = jnp.power(ROPE_BASE, -(2.0 * jnp.arange(half_dim, dtype=jnp.float32)) / HEAD_SIZE)
    angles = doc_positions(segments).astype(jnp.float32)[..., None] * frequency
    cosine_table = jnp.concatenate([jnp.cos(angles), jnp.cos(angles)], axis=-1)
    sine_table = jnp.concatenate([jnp.sin(angles), jnp.sin(angles)], axis=-1)
    return (cosine_table, sine_table)


def rotate(vector, cosine_table, sine_table):
    half_dim = vector.shape[-1] // 2
    turned = jnp.concatenate([-vector[..., half_dim:], vector[..., :half_dim]], axis=-1)
    return vector * cosine_table + turned * sine_table


def unrotate(vector, cosine_table, sine_table):
    half_dim = vector.shape[-1] // 2
    shifted = vector * sine_table
    returned = jnp.concatenate([shifted[..., half_dim:], -shifted[..., :half_dim]], axis=-1)
    return vector * cosine_table + returned


def allowed_pairs(segments):
    length = segments.shape[1]
    offsets = jnp.arange(length)
    causal = offsets[None, :] <= offsets[:, None]
    same_doc = segments[:, :, None] == segments[:, None, :]
    return (causal[None] & same_doc)[:, None, None]


def score_block(queries, key_heads, segments):
    scores = jnp.einsum(
        "sqgrd,skgd->sgrqk", queries, key_heads, preferred_element_type=jnp.float32
    ) * HEAD_SIZE ** (-0.5)
    return jnp.where(allowed_pairs(segments), scores, NEG_FILL)


def rms_scale(features):
    return lax.rsqrt(jnp.mean(features * features, axis=-1, keepdims=True) + EPS)


def norm_back(features, inverse, gain_vector, upstream):
    scaled = gain_vector * upstream
    return inverse * scaled - features * (inverse * inverse * inverse) * jnp.mean(
        scaled * features, axis=-1, keepdims=True
    )


def widen(shard_rows):
    return lax.all_gather(shard_rows, "tensor", axis=0, tiled=True)


def narrow(partial_value):
    return lax.psum_scatter(
        partial_value.astype(jnp.bfloat16), "tensor", scatter_dimension=0, tiled=True
    ).astype(jnp.float32)


def local(
    block_in,
    cotangent,
    segment_ids,
    attn_gain,
    qkv_weight,
    out_weight,
    mlp_gain,
    gate_weight,
    up_weight,
    down_weight,
):
    qkv_full, gate_full, up_full, gain_attn_raw, gain_mlp_raw = (
        lax.all_gather(qkv_weight, "dp", axis=0, tiled=True),
        lax.all_gather(gate_weight, "dp", axis=0, tiled=True),
        lax.all_gather(up_weight, "dp", axis=0, tiled=True),
        lax.all_gather(attn_gain, "dp", axis=0, tiled=True),
        lax.all_gather(mlp_gain, "dp", axis=0, tiled=True),
    )
    out_cols, down_cols = (
        lax.all_gather(out_weight, "dp", axis=1, tiled=True),
        lax.all_gather(down_weight, "dp", axis=1, tiled=True),
    )
    seq_count, length = segment_ids.shape
    repeat_factor = QUERY_HEADS // KEY_VALUE_HEADS
    groups = qkv_full.shape[1] // ((repeat_factor + 2) * HEAD_SIZE)
    gain_attn = gain_attn_raw.astype(jnp.float32)
    gain_mlp = gain_mlp_raw.astype(jnp.float32)
    residual = block_in.astype(jnp.float32)
    scale_attn = rms_scale(residual)
    normed1 = widen((residual * scale_attn * gain_attn).astype(jnp.bfloat16))
    projected = jnp.dot(normed1, qkv_full, preferred_element_type=jnp.float32).reshape(
        seq_count, length, groups, repeat_factor + 2, HEAD_SIZE
    )
    cosine_table, sine_table = rotary_tables(segment_ids)
    cos_query = cosine_table[:, :, None, None, :]
    sin_query = sine_table[:, :, None, None, :]
    cos_key = cosine_table[:, :, None, :]
    sin_key = sine_table[:, :, None, :]
    queries = rotate(projected[:, :, :, :repeat_factor], cos_query, sin_query).astype(jnp.bfloat16)
    key_heads = rotate(projected[:, :, :, repeat_factor], cos_key, sin_key).astype(jnp.bfloat16)
    values = projected[:, :, :, repeat_factor + 1].astype(jnp.bfloat16)
    scores = score_block(queries, key_heads, segment_ids)
    highest = jnp.max(scores, axis=-1, keepdims=True)
    log_total = highest + jnp.log(jnp.sum(jnp.exp(scores - highest), axis=-1, keepdims=True))
    probability = jnp.exp(scores - log_total).astype(jnp.bfloat16)
    attended = jnp.einsum(
        "sgrqk,skgd->sqgrd", probability, values, preferred_element_type=jnp.float32
    ).astype(jnp.bfloat16)
    attn_flat = attended.reshape(seq_count * length, groups * repeat_factor * HEAD_SIZE)
    attn_delta = lax.psum_scatter(
        jnp.dot(attn_flat, out_cols, preferred_element_type=jnp.float32).astype(jnp.bfloat16),
        "tensor",
        scatter_dimension=0,
        tiled=True,
    ).astype(jnp.float32)
    hidden1 = residual + attn_delta
    scale_mlp = rms_scale(hidden1)
    normed2 = widen((hidden1 * scale_mlp * gain_mlp).astype(jnp.bfloat16))
    gate = jnp.dot(normed2, gate_full, preferred_element_type=jnp.float32)
    up_value = jnp.dot(normed2, up_full, preferred_element_type=jnp.float32)
    sigmoid_gate = jax.nn.sigmoid(gate)
    activated = (gate * sigmoid_gate * up_value).astype(jnp.bfloat16)
    mlp_delta = narrow(jnp.dot(activated, down_cols, preferred_element_type=jnp.float32))
    block_out = (hidden1 + mlp_delta).astype(jnp.bfloat16)
    grad_rows = widen(cotangent)
    down_part = jnp.einsum("tf,td->fd", activated, grad_rows, preferred_element_type=jnp.float32)
    act_grad = jnp.einsum("td,fd->tf", grad_rows, down_cols, preferred_element_type=jnp.float32)
    gate_delta = (act_grad * up_value * sigmoid_gate * (1.0 + gate * (1.0 - sigmoid_gate))).astype(
        jnp.bfloat16
    )
    up_delta = (act_grad * gate * sigmoid_gate).astype(jnp.bfloat16)
    gate_part = jnp.einsum("td,tf->df", normed2, gate_delta, preferred_element_type=jnp.float32)
    up_part = jnp.einsum("td,tf->df", normed2, up_delta, preferred_element_type=jnp.float32)
    normed2_term = jnp.einsum(
        "tf,df->td", gate_delta, gate_full, preferred_element_type=jnp.float32
    ) + jnp.einsum("tf,df->td", up_delta, up_full, preferred_element_type=jnp.float32)
    normed2_grad = narrow(normed2_term)
    mlp_gain_part = jnp.sum(normed2_grad * hidden1 * scale_mlp, axis=0)
    hidden1_grad = cotangent.astype(jnp.float32) + norm_back(
        hidden1, scale_mlp, gain_mlp, normed2_grad
    )
    hidden1_rounded = hidden1_grad.astype(jnp.bfloat16)
    grad_full = lax.all_gather(hidden1_rounded, "tensor", axis=0, tiled=True)
    attended_grad = jnp.einsum(
        "td,hd->th", grad_full, out_cols, preferred_element_type=jnp.float32
    ).astype(jnp.bfloat16)
    out_part = jnp.einsum("th,td->hd", attn_flat, grad_full, preferred_element_type=jnp.float32)
    attended_grad = attended_grad.reshape(seq_count, length, groups, repeat_factor, HEAD_SIZE)
    prob_full = jnp.exp(score_block(queries, key_heads, segment_ids) - log_total)
    prob_grad = jnp.einsum(
        "sqgrd,skgd->sgrqk", attended_grad, values, preferred_element_type=jnp.float32
    )
    inner_sum = jnp.sum(prob_full * prob_grad, axis=-1, keepdims=True)
    score_grad = (prob_full * (prob_grad - inner_sum) * HEAD_SIZE ** (-0.5)).astype(jnp.bfloat16)
    query_grad = jnp.einsum(
        "sgrqk,skgd->sqgrd", score_grad, key_heads, preferred_element_type=jnp.float32
    )
    key_grad = jnp.einsum(
        "sgrqk,sqgrd->skgd", score_grad, queries, preferred_element_type=jnp.float32
    )
    value_grad = jnp.einsum(
        "sgrqk,sqgrd->skgd",
        prob_full.astype(jnp.bfloat16),
        attended_grad,
        preferred_element_type=jnp.float32,
    )
    projected_grad = jnp.concatenate(
        [
            unrotate(query_grad, cos_query, sin_query),
            unrotate(key_grad, cos_key, sin_key)[:, :, :, None],
            value_grad[:, :, :, None],
        ],
        axis=3,
    )
    projected_grad = projected_grad.astype(jnp.bfloat16).reshape(
        seq_count * length, groups * (repeat_factor + 2) * HEAD_SIZE
    )
    qkv_part = jnp.einsum("td,tc->dc", normed1, projected_grad, preferred_element_type=jnp.float32)
    normed1_grad = narrow(
        jnp.einsum("tc,dc->td", projected_grad, qkv_full, preferred_element_type=jnp.float32)
    )
    attn_gain_part = jnp.sum(normed1_grad * residual * scale_attn, axis=0)
    input_grad = (hidden1_grad + norm_back(residual, scale_attn, gain_attn, normed1_grad)).astype(
        jnp.bfloat16
    )
    attn_gain_total, mlp_gain_total = lax.psum((attn_gain_part, mlp_gain_part), "tensor")
    attn_gain_grad, qkv_grad, gate_grad, up_grad, mlp_gain_grad = (
        lax.psum_scatter(
            attn_gain_total.astype(jnp.bfloat16), "dp", scatter_dimension=0, tiled=True
        ).astype(jnp.float32),
        lax.psum_scatter(
            qkv_part.astype(jnp.bfloat16), "dp", scatter_dimension=0, tiled=True
        ).astype(jnp.float32),
        lax.psum_scatter(
            gate_part.astype(jnp.bfloat16), "dp", scatter_dimension=0, tiled=True
        ).astype(jnp.float32),
        lax.psum_scatter(
            up_part.astype(jnp.bfloat16), "dp", scatter_dimension=0, tiled=True
        ).astype(jnp.float32),
        lax.psum_scatter(
            mlp_gain_total.astype(jnp.bfloat16), "dp", scatter_dimension=0, tiled=True
        ).astype(jnp.float32),
    )
    out_grad, down_grad = (
        lax.psum_scatter(
            out_part.astype(jnp.bfloat16), "dp", scatter_dimension=1, tiled=True
        ).astype(jnp.float32),
        lax.psum_scatter(
            down_part.astype(jnp.bfloat16), "dp", scatter_dimension=1, tiled=True
        ).astype(jnp.float32),
    )
    return (
        block_out,
        input_grad,
        attn_gain_grad,
        qkv_grad,
        out_grad,
        mlp_gain_grad,
        gate_grad,
        up_grad,
        down_grad,
    )


GROUP = 4
WINDOW = 256
LANES = 384
TILE = 128


MESH = pl.DeviceIdType.MESH


class Transfer:
    def __init__(self, copy, sends=None, receives=None):
        self.copy, self.sends, self.receives = copy, sends, receives

    def _when(self, condition, action):
        if condition is None:
            action()
        else:
            pl.when(condition)(action)

    def start(self):
        self._when(self.sends, self.copy.start)
        return self

    def wait_recv(self):
        self._when(self.receives, self.copy.wait_recv)

    def wait_send(self):
        self._when(self.sends, self.copy.wait_send)


class Links:
    def __init__(self, n_dp, n_tensor, out_sems, in_sems, local_sems):
        self.n_dp, self.n_tensor = n_dp, n_tensor
        self.out_sems, self.in_sems, self.local_sems = out_sems, in_sems, local_sems
        self.d_at, self.z_at = lax.axis_index("dp"), lax.axis_index("tensor")
        self.used, self.used_local = 0, 0
        self.sent, self.saved = [], []

    def barrier(self):
        barrier = pltpu.get_barrier_semaphore()
        for k in range(1, self.n_dp):
            pl.semaphore_signal(
                barrier,
                inc=1,
                device_id={"dp": self.d_at ^ k, "tensor": self.z_at},
                device_id_type=MESH,
            )
        for s in range(1, self.n_tensor):
            pl.semaphore_signal(
                barrier,
                inc=1,
                device_id={"dp": self.d_at, "tensor": lax.rem(self.z_at + s, self.n_tensor)},
                device_id_type=MESH,
            )
        pl.semaphore_wait(barrier, self.n_dp - 1 + self.n_tensor - 1)

    def plan(self, source, target, bit=0, shift=0, sends=None, receives=None):
        slot = self.used
        self.used += 1
        copy = pltpu.make_async_remote_copy(
            src_ref=source,
            dst_ref=target,
            send_sem=self.out_sems.at[slot],
            recv_sem=self.in_sems.at[slot],
            device_id={
                "dp": self.d_at ^ bit,
                "tensor": lax.rem(self.z_at + self.n_tensor + shift, self.n_tensor),
            },
            device_id_type=MESH,
        )
        transfer = Transfer(copy, sends, receives)
        self.sent.append(transfer)
        return transfer

    def send(self, source, target, bit=0, shift=0):
        return self.plan(source, target, bit, shift).start()

    def move(self, source, target):
        copy = pltpu.make_async_copy(source, target, self.local_sems.at[self.used_local])
        self.used_local += 1
        copy.start()
        return copy

    def save(self, source, target):
        self.saved.append(self.move(source, target))

    def finish(self):
        for transfer in self.sent:
            transfer.wait_send()
        for copy in self.saved:
            copy.wait()


class Spread:
    def __init__(self, links, own_piece, target, columns):
        self.links, self.own_piece, self.target, self.columns = links, own_piece, target, columns
        self.ahead, self.back, self.swaps = [], [], []

    def _slot(self, index):
        n = self.links.n_tensor
        return self.target.at[lax.rem(index + n, n), :, self.columns]

    def issue(self):
        links, n, z = self.links, self.links.n_tensor, self.links.z_at
        own = self._slot(z)
        for s in range(1, n):
            up_from, down_from = z - (s - 1), z + (s - 1)
            up_source = self.own_piece if s == 1 else self._slot(up_from)
            down_source = self.own_piece if s == 1 else self._slot(down_from)
            self.ahead.append(
                links.plan(
                    up_source, self._slot(up_from), shift=1,
                    sends=(z < n - 1) & (up_from >= 0), receives=z >= s,
                )
            )
            self.back.append(
                links.plan(
                    down_source, self._slot(down_from), shift=-1,
                    sends=(z > 0) & (down_from < n), receives=z + s < n,
                )
            )
        self.ahead[0].start()
        self.back[0].start()
        self.swaps.append(links.plan(self.own_piece, own, bit=GROUP).start())

    def step(self, s):
        links, n, z = self.links, self.links.n_tensor, self.links.z_at
        for arrivals, piece, here in (
            (self.ahead, z - s, z >= s),
            (self.back, z + s, z + s < n),
        ):
            arrivals[s - 1].wait_recv()
            if s < n - 1:
                arrivals[s].start()
            slot = self._slot(piece)
            self.swaps.append(
                links.plan(slot, slot, bit=GROUP, sends=here, receives=here).start()
            )

    def wait(self):
        for swap in self.swaps:
            swap.wait_recv()


def kernel_forward(
    n_dp, n_tensor,
    tokens, cot, out_w, gate_w, up_w, down_w, qkv_w, segments, gain_rows, fixed,
    normed1_out, normed2_out, hidden_out, query_out, keyval_out, log_out, att_out,
    cos_out, sin_out, qkv_out, out_out, small_out, cot_out, gate_out, up_out, down_out,
    x_all, n1_all, first, dealt, first_piece, qkv, obuf, gbuf, ubuf, dbuf, piece, outw,
    small, small_all, stream, parts, recv, queries, keyvals,
    att, by_repeat, logs, cosine, sine, low_col, to_core, from_core, to_across, from_across,
    hidden, n2_all, stage, out_sems, in_sems, local_sems,
):
    f32, bf16 = jnp.float32, jnp.bfloat16
    links = Links(n_dp, n_tensor, out_sems, in_sems, local_sems)
    send, move, save = links.send, links.move, links.save
    d_at, z_at = links.d_at, links.z_at
    member = d_at % GROUP
    core = d_at % 2
    upper = d_at // GROUP
    rows, width = tokens.shape
    half = width // 2
    chunk = qkv_w.shape[0]
    contract = (((1,), (1,)), ((), ()))
    columns = pl.ds(pl.multiple_of(upper * half, half), half)

    turned = qkv_w[...].T
    quarter = turned.shape[0] // GROUP
    for i in range(GROUP):
        first[i] = turned[i * quarter : (i + 1) * quarter]
    ids = segments[...]
    seqs, length = ids.shape
    begin = jnp.zeros_like(ids)
    for value in range(3):
        count = jnp.sum((ids == value).astype(jnp.int32), axis=1, keepdims=True)
        begin = begin + jnp.where(ids > value, count, 0)
    begin = begin.astype(f32)
    for i in range(seqs):
        stream[:, i * length : (i + 1) * length] = jnp.broadcast_to(
            begin[i : i + 1] + float(i * length), (stream.shape[0], length)
        )
    window = stream[:, pl.ds(pl.multiple_of(z_at * rows, TILE), rows)]
    here = lax.broadcasted_iota(jnp.int32, window.shape, 1) + z_at * rows
    small[...] = window
    small[0:1] = here.astype(f32)[0:1] - window[0:1]
    small[2:4, :chunk] = gain_rows[...].astype(f32)

    @pl.when(z_at == 0)
    def _():
        keyvals[:, :WINDOW, :] = jnp.zeros_like(keyvals[:, :WINDOW, :])

    links.barrier()

    deals = [send(first.at[member ^ k], dealt.at[member], bit=k) for k in range(1, GROUP)]
    beside = send(tokens, x_all.at[2], bit=1)
    smalls = [send(small, small_all.at[d_at], bit=k) for k in range(1, n_dp)]
    rests = []

    def rows_of(ref, at):
        size = ref.shape[0] // GROUP
        return ref.at[pl.ds(pl.multiple_of(at * size, 16), size), :]

    def columns_of(ref, at):
        size = ref.shape[1] // GROUP
        return ref.at[:, pl.ds(pl.multiple_of(at * size, TILE), size)]

    pairs = [(out_w, obuf, rows_of), (gate_w, gbuf, columns_of), (up_w, ubuf, columns_of)]
    pairs.append((down_w, dbuf, rows_of))
    for ref, buffer, take in pairs:
        for k in range(1, GROUP):
            rests.append(send(take(ref, member ^ k), buffer.at[member], bit=k))
    own = [move(tokens, x_all.at[0])]
    for ref, buffer, take in pairs:
        own.append(move(take(ref, member), buffer.at[member]))
    cot_stage = move(cot, stage)
    small_all[d_at] = small[...]
    dealt[member] = first[member]

    entries = lax.broadcasted_iota(jnp.int32, (WINDOW, LANES), 0).astype(f32)
    angles = entries * fixed[0:1]

    def split(table):
        pieces = []
        for _ in range(3):
            pieces.append(table.astype(bf16))
            table = table - pieces[-1].astype(f32)
        return pieces

    cos_parts, sin_parts = split(jnp.cos(angles)), split(jnp.sin(angles))
    second = fixed[1:2]
    own_turns = jnp.where(core == 0, jnp.ones_like(second), fixed[2:3])

    for copy in deals:
        copy.wait_recv()
    for i in range(GROUP):
        first_piece[:, i * chunk : (i + 1) * chunk] = dealt[i]
    spread_first = Spread(links, first_piece, qkv, columns)
    spread_first.issue()
    save(first_piece, qkv.at[z_at, :, columns])
    own_qkv = links.saved.pop()
    for copy in own:
        copy.wait()
    cot_stage.wait()
    save(stage, cot_out.at[0])
    spread_first.step(1)
    for copy in smalls:
        copy.wait_recv()
    spread_first.step(2)
    gains = []
    for row in (2, 3):
        gains.append(
            jnp.concatenate([small_all[i, row : row + 1, :chunk] for i in range(n_dp)], axis=1)
        )
    for copy in rests:
        copy.wait_recv()
    across = send(tokens, x_all.at[1], bit=2)
    sizes = [obuf.shape[1], gbuf.shape[2], ubuf.shape[2], dbuf.shape[1]]
    starts = [sum(sizes[:i]) for i in range(len(sizes))]
    spreads = []
    for index, (target, buffer) in enumerate(
        ((outw, obuf), (gate_out, gbuf), (up_out, ubuf), (down_out, dbuf))
    ):
        at = slice(starts[index], starts[index] + sizes[index])
        for i in range(GROUP):
            value = buffer[i]
            piece[at, i * chunk : (i + 1) * chunk] = (
                value.T if value.shape[0] == chunk and sizes[index] != chunk else value
            )
        own_piece = piece.at[pl.ds(starts[index], sizes[index])]
        spreads.append(Spread(links, own_piece, target, columns))
    out_spread, gate_spread, up_spread, down_spread = spreads
    saves = [move(s.own_piece, s.target.at[z_at, :, columns]) for s in spreads]
    out_spread.issue()
    spread_first.step(3)
    gate_spread.issue()
    beside.wait_recv()
    own_qkv.wait()
    spread_first.wait()

    def project_block(m, k):
        features = x_all[m].astype(f32)
        scale = lax.rsqrt(jnp.mean(features * features, axis=1, keepdims=True) + EPS)
        normal = (features * scale * gains[0]).astype(bf16)
        n1_all[m] = normal
        units = qkv.shape[0] * qkv.shape[1]
        product = lax.dot_general(
            normal, qkv[...].reshape(units, width), contract, preferred_element_type=f32
        )
        info = small_all[d_at ^ k].T
        key = lax.broadcasted_iota(jnp.int32, (rows, WINDOW), 1)
        chosen = (info[:, 0:1].astype(jnp.int32) == key).astype(bf16)

        def pick(table):
            total = jnp.dot(chosen, table[0], preferred_element_type=f32)
            for part in table[1:]:
                total += jnp.dot(chosen, part, preferred_element_type=f32)
            return total

        cos_here, sin_here = pick(cos_parts), pick(sin_parts)
        parts[m] = turn(product, cos_here, sin_here, second, own_turns, 1.0).astype(bf16)
        if m < 2:
            cosine[m] = cos_here
            sine[m] = sin_here
            low_col[m] = info[:, 1:2].astype(jnp.int32) - z_at * rows + WINDOW

    is_first = core == 0
    halos = [
        links.plan(
            keyvals.at[m, pl.ds(rows, WINDOW)], keyvals.at[m, pl.ds(0, WINDOW)], shift=1,
            sends=z_at < n_tensor - 1, receives=z_at > 0,
        )
        for m in range(2)
    ]

    def take_block(m, swap):
        swap.wait_recv()
        mine, other = parts[m], recv[m]
        queries[m] = jnp.where(is_first, mine, other)
        keyvals[m, WINDOW:, :] = jnp.where(is_first, other, mine)
        halos[m].start()

    project_block(2, 1)
    part_swap = send(parts.at[2], recv.at[0], bit=1)
    project_block(0, 0)
    take_block(0, part_swap)
    out_spread.step(1)
    across.wait_recv()
    both = send(x_all.at[1], x_all.at[3], bit=1)
    cot_across = send(cot, cot_out.at[1], bit=2)
    cot_beside = send(cot, cot_out.at[2], bit=1)
    out_spread.step(2)
    project_block(1, 2)
    both.wait_recv()
    project_block(3, 3)
    part_swap = send(parts.at[3], recv.at[1], bit=1)
    out_spread.step(3)
    save(n1_all, normed1_out)
    save(cosine, cos_out)
    save(sine, sin_out)
    take_block(1, part_swap)
    gate_spread.step(1)
    save(queries, query_out)
    heads = queries.shape[2] // HEAD_SIZE
    repeat = QUERY_HEADS // KEY_VALUE_HEADS
    span = TILE + WINDOW

    def attend_tile(m, start):
        key = lax.broadcasted_iota(jnp.int32, (TILE, span), 1)
        query = lax.broadcasted_iota(jnp.int32, (TILE, span), 0)
        lowest = low_col[m, pl.ds(start, TILE), :] - start
        allowed = (key >= lowest) & (key <= query + WINDOW)
        for head in range(heads):
            group, r = head // repeat, head % repeat
            base = group * 2 * HEAD_SIZE
            q = queries[m, pl.ds(start, TILE), head * HEAD_SIZE : (head + 1) * HEAD_SIZE]
            k = keyvals[m, pl.ds(start, span), base : base + HEAD_SIZE]
            v = keyvals[m, pl.ds(start, span), base + HEAD_SIZE : base + 2 * HEAD_SIZE]
            s = lax.dot_general(q, k, contract, preferred_element_type=f32) * HEAD_SIZE ** (-0.5)
            s = jnp.where(allowed, s, NEG_FILL)
            highest = jnp.max(s, axis=1, keepdims=True)
            e = jnp.exp(s - highest)
            whole = jnp.sum(e, axis=1, keepdims=True)
            p = (e * (1.0 / whole)).astype(bf16)
            o = jnp.dot(p, v, preferred_element_type=f32).astype(bf16)
            logs[m, pl.ds(start, TILE), head : head + 1] = highest + jnp.log(whole)
            by_repeat[r, m, pl.ds(start, TILE), group * HEAD_SIZE : (group + 1) * HEAD_SIZE] = o

    tiles = rows // TILE
    free = -(-WINDOW // TILE)
    for tile in range(free, tiles):
        attend_tile(1, tile * TILE)
        attend_tile(0, tile * TILE)
    gate_spread.step(2)
    halos[0].wait_recv()
    halos[1].wait_recv()
    up_spread.issue()
    for tile in range(free):
        attend_tile(1, tile * TILE)
    att_swap1 = send(by_repeat.at[1 - core, 1], att.at[3], bit=1)
    gate_spread.step(3)
    attend_tile(0, 0)
    up_spread.step(1)
    for tile in range(1, free):
        attend_tile(0, tile * TILE)
    att_swap0 = send(by_repeat.at[1 - core, 0], att.at[2], bit=1)
    save(keyvals, keyval_out)
    save(logs, log_out)
    att[0] = by_repeat[core, 0]
    att[1] = by_repeat[core, 1]
    down_spread.issue()
    cot_across.wait_recv()
    cot_both = send(cot_out.at[1], cot_out.at[3], bit=1)

    saves[0].wait()
    out_spread.wait()

    def project_out(b):
        units = outw.shape[0] * outw.shape[1]
        return jnp.dot(att[b], outw[...].reshape(units, width), preferred_element_type=f32)

    att_swap1.wait_recv()
    to_core[1] = project_out(3).astype(bf16)
    core_send1 = send(to_core.at[1], from_core.at[1], bit=1)
    hidden[...] = project_out(1)
    att_swap0.wait_recv()
    to_core[0] = project_out(2).astype(bf16)
    core_send0 = send(to_core.at[0], from_core.at[0], bit=1)
    core_send1.wait_recv()
    across_sends = []
    for i in range(tiles):
        at = pl.ds(i * TILE, TILE)
        to_across[at] = (hidden[at, :] + from_core[1, at, :].astype(f32)).astype(bf16)
        across_sends.append(send(to_across.at[at], from_across.at[at], bit=2))
    hidden[...] = project_out(0) + x_all[0].astype(f32)
    core_send0.wait_recv()
    hidden[...] += from_core[0].astype(f32)
    save(att, att_out)
    up_spread.step(2)
    steps = [(up_spread, 3), (down_spread, 1), (down_spread, 2), (down_spread, 3)]
    last = []
    for i in range(tiles):
        at = pl.ds(i * TILE, TILE)
        across_sends[i].wait_recv()
        value = hidden[at, :] + from_across[at, :].astype(f32)
        hidden[at, :] = value
        scale = lax.rsqrt(jnp.mean(value * value, axis=1, keepdims=True) + EPS)
        n2_all[0, at, :] = (value * scale * gains[1]).astype(bf16)
        last.append(send(n2_all.at[0, at], n2_all.at[1, at], bit=2))
        last.append(send(n2_all.at[0, at], n2_all.at[2, at], bit=1))
        if i in (1, 2):
            spread, s = steps.pop(0)
            spread.step(s)
    save(hidden, hidden_out)
    save(qkv, qkv_out)
    save(outw, out_out)
    save(small_all, small_out)
    ends = []
    for i in range(tiles):
        at = pl.ds(i * TILE, TILE)
        last[2 * i].wait_recv()
        ends.append(send(n2_all.at[1, at], n2_all.at[3, at], bit=1))
        if i < 2:
            spread, s = steps.pop(0)
            spread.step(s)
    for copy in ends + last[1::2]:
        copy.wait_recv()
    save(n2_all, normed2_out)
    for copy in saves[1:]:
        copy.wait()
    for spread in (gate_spread, up_spread, down_spread):
        spread.wait()
    for copy in (cot_beside, cot_both):
        copy.wait_recv()
    links.finish()


def forward(
    n_dp, n_tensor, tokens, cot, segments, gain_rows, qkv_w, out_w, gate_w, up_w, down_w
):
    rows, width = tokens.shape
    f32, bf16 = jnp.float32, jnp.bfloat16
    vmem = pl.BlockSpec(memory_space=pltpu.VMEM)
    hbm = pl.BlockSpec(memory_space=pl.ANY)
    chunk = qkv_w.shape[0]
    quarter = qkv_w.shape[1] // GROUP
    sizes = [
        out_w.shape[0] // GROUP, gate_w.shape[1] // GROUP, up_w.shape[1] // GROUP,
        down_w.shape[0] // GROUP,
    ]
    units = quarter * n_tensor
    heads = units // HEAD_SIZE
    lane = np.arange(LANES)
    within = lane % HEAD_SIZE
    fixed = np.zeros((8, LANES), np.float32)
    fixed[0] = np.power(ROPE_BASE, -(2.0 * (within % (HEAD_SIZE // 2))) / HEAD_SIZE)
    fixed[1] = within >= HEAD_SIZE // 2
    fixed[2] = lane % (2 * HEAD_SIZE) < HEAD_SIZE
    fixed[3] = 1.0

    def shape(dims, dtype=bf16):
        return jax.ShapeDtypeStruct(tuple(dims), dtype)

    full = (GROUP, rows, width)
    qkv_shape = (n_tensor, quarter, width)
    out_shape = (n_tensor, sizes[0], width)
    att_shape = (GROUP, rows, units // 2)
    small_shape = (n_dp, 8, rows)
    table = (2, rows, LANES)
    outs = [
        shape(full),
        shape(full),
        shape((rows, width), f32),
        shape((2, rows, units)),
        shape((2, rows + WINDOW, units)),
        shape((2, rows, heads), f32),
        shape(att_shape),
        shape(table, f32),
        shape(table, f32),
        shape(qkv_shape),
        shape(out_shape),
        shape(small_shape, f32),
        shape(full),
    ] + [shape((n_tensor, size, width)) for size in sizes[1:]]
    scratch = [
        pltpu.VMEM(full, bf16),
        pltpu.VMEM(full, bf16),
        pltpu.VMEM((GROUP, quarter, chunk), bf16),
        pltpu.VMEM((GROUP, quarter, chunk), bf16),
        pltpu.VMEM((quarter, width // 2), bf16),
        pltpu.VMEM(qkv_shape, bf16),
        pltpu.VMEM((GROUP, sizes[0], chunk), bf16),
        pltpu.VMEM((GROUP, chunk, sizes[1]), bf16),
        pltpu.VMEM((GROUP, chunk, sizes[2]), bf16),
        pltpu.VMEM((GROUP, sizes[3], chunk), bf16),
        pltpu.VMEM((sum(sizes), width // 2), bf16),
        pltpu.VMEM(out_shape, bf16),
        pltpu.VMEM((8, rows), f32),
        pltpu.VMEM(small_shape, f32),
        pltpu.VMEM((8, n_tensor * rows), f32),
        pltpu.VMEM((GROUP, rows, units), bf16),
        pltpu.VMEM((2, rows, units), bf16),
        pltpu.VMEM((2, rows, units), bf16),
        pltpu.VMEM((2, rows + WINDOW, units), bf16),
        pltpu.VMEM(att_shape, bf16),
        pltpu.VMEM((2, 2, rows, units // 2), bf16),
        pltpu.VMEM((2, rows, heads), f32),
        pltpu.VMEM(table, f32),
        pltpu.VMEM(table, f32),
        pltpu.VMEM((2, rows, 1), jnp.int32),
        pltpu.VMEM((2, rows, width), bf16),
        pltpu.VMEM((2, rows, width), bf16),
        pltpu.VMEM((rows, width), bf16),
        pltpu.VMEM((rows, width), bf16),
        pltpu.VMEM((rows, width), f32),
        pltpu.VMEM(full, bf16),
        pltpu.VMEM((rows, width), bf16),
        pltpu.SemaphoreType.DMA((128,)),
        pltpu.SemaphoreType.DMA((128,)),
        pltpu.SemaphoreType.DMA((40,)),
    ]
    results = pl.pallas_call(
        functools.partial(kernel_forward, n_dp, n_tensor),
        in_specs=[hbm] * 6 + [vmem] * 4,
        out_specs=[hbm] * len(outs),
        out_shape=outs,
        scratch_shapes=scratch,
        compiler_params=pltpu.CompilerParams(
            collective_id=0, has_side_effects=True, vmem_limit_bytes=60 * 1024 * 1024
        ),
        name="forward",
    )(
        tokens, cot, out_w, gate_w, up_w, down_w, qkv_w, segments, gain_rows, jnp.asarray(fixed)
    )
    return results, jnp.asarray(fixed)


def turn(value, cosine, sine, second, turns, sign):
    width = value.shape[1]
    half = HEAD_SIZE // 2
    c = turns * cosine + (1.0 - turns)
    u = (sign * turns * second) * sine
    d = (sign * turns * (second - 1.0)) * sine
    pieces = []
    up = pltpu.roll(value, half, 1)
    down = pltpu.roll(value, width - half, 1)
    for i in range(width // LANES):
        at = slice(i * LANES, (i + 1) * LANES)
        pieces.append(value[:, at] * c + up[:, at] * u + down[:, at] * d)
    return jnp.concatenate(pieces, axis=1)


def kernel_feed(
    n_dp, n_tensor,
    n2_in, cot_in, hidden_in, gate_in, up_in, down_in, smalls,
    grad_out, grad_own_out, mlp_out, down_out, gate_out, up_out, down_got, row_out,
    n2_all, cot_all, gate_w, up_w, down_w, active, gate_delta, up_delta,
    down_part, gate_part, up_part, to_core, from_core, to_across, from_across, hidden, total,
    rounded, row, out_sems, in_sems, local_sems,
):
    f32, bf16 = jnp.float32, jnp.bfloat16
    links = Links(n_dp, n_tensor, out_sems, in_sems, local_sems)
    send, move, save = links.send, links.move, links.save
    upper = links.d_at // GROUP
    rows, width = hidden.shape
    half = width // 2
    chunk = width // n_dp
    size = gate_w.shape[1]
    units = n_tensor * size
    contract = (((1,), (1,)), ((), ()))
    over_rows = (((0,), (0,)), ((), ()))
    other = pl.ds(pl.multiple_of((1 - upper) * half, half), half)
    tiles = rows // TILE

    loads = [
        move(gate_in, gate_w), move(n2_in, n2_all), move(up_in, up_w), move(down_in, down_w),
        move(cot_in, cot_all), move(hidden_in, hidden),
    ]
    links.barrier()
    for copy in loads[:-1]:
        copy.wait()

    def inner(i, carry):
        m, p = i // n_tensor, i % n_tensor
        at = pl.ds(pl.multiple_of(p * size, TILE), size)
        gate = lax.dot_general(n2_all[m], gate_w[p], contract, preferred_element_type=f32)
        up_value = lax.dot_general(n2_all[m], up_w[p], contract, preferred_element_type=f32)
        act_grad = lax.dot_general(cot_all[m], down_w[p], contract, preferred_element_type=f32)
        sigmoid = jax.nn.sigmoid(gate)
        silu = gate * sigmoid
        active[m, :, at] = (silu * up_value).astype(bf16)
        gate_delta[m, :, at] = (
            act_grad * up_value * sigmoid * (1.0 + gate * (1.0 - sigmoid))
        ).astype(bf16)
        up_delta[m, :, at] = (act_grad * silu).astype(bf16)
        return carry

    lax.fori_loop(0, GROUP * n_tensor, inner, 0)

    def back(m):
        return jnp.dot(
            gate_delta[m], gate_w[...].reshape(units, width), preferred_element_type=f32
        ) + jnp.dot(up_delta[m], up_w[...].reshape(units, width), preferred_element_type=f32)

    to_core[1] = back(3).astype(bf16)
    core_send1 = send(to_core.at[1], from_core.at[1], bit=1)
    total[...] = back(1)
    core_send1.wait_recv()
    across = []
    for i in range(tiles):
        at = pl.ds(i * TILE, TILE)
        to_across[at] = (total[at, :] + from_core[1, at, :].astype(f32)).astype(bf16)
        across.append(send(to_across.at[at], from_across.at[at], bit=2))
    to_core[0] = back(2).astype(bf16)
    core_send0 = send(to_core.at[0], from_core.at[0], bit=1)
    total[...] = back(0)

    order = []
    for i in range((n_tensor + 1) // 2):
        order.extend(dict.fromkeys((n_tensor - 1 - i, i)))

    def grads(left, right, part, target, weight=None):
        for p in order:
            at = slice(p * size, (p + 1) * size)
            grad = lax.dot_general(
                left[...].reshape(GROUP * rows, units)[:, at],
                right[...].reshape(GROUP * rows, width),
                over_rows,
                preferred_element_type=f32,
            )
            part[p] = grad.astype(bf16)
            if weight is not None:
                row[...] += jnp.sum(grad * weight[p].astype(f32), axis=0, keepdims=True)
            else:
                swaps.append(send(part.at[p, :, other], down_got.at[p], bit=GROUP))
            save(part.at[p], target.at[p])

    swaps = []
    row[...] = jnp.zeros_like(row)
    grads(active, cot_all, down_part, down_out)
    core_send0.wait_recv()
    total[...] += from_core[0].astype(f32)
    grads(gate_delta, n2_all, gate_part, gate_out, gate_w)
    grads(up_delta, n2_all, up_part, up_out, up_w)
    save(row, row_out)
    for m in range(GROUP):
        n2_all[m] = jnp.dot(
            active[m], down_w[...].reshape(units, width), preferred_element_type=f32
        ).astype(bf16)
        save(n2_all.at[m], mlp_out.at[m])
    gain = jnp.concatenate([smalls[i, 3:4, :chunk] for i in range(n_dp)], axis=1)
    loads[-1].wait()
    for i in range(tiles):
        at = pl.ds(i * TILE, TILE)
        across[i].wait_recv()
        upstream = total[at, :] + from_across[at, :].astype(f32)
        features = hidden[at, :]
        inverse = lax.rsqrt(jnp.mean(features * features, axis=1, keepdims=True) + EPS)
        scaled = gain * upstream
        mean = jnp.mean(scaled * features, axis=1, keepdims=True)
        result = cot_all[0, at, :].astype(f32) + (
            inverse * scaled - features * (inverse * inverse * inverse) * mean
        )
        total[at, :] = result
        rounded[at, :] = result.astype(bf16)
    save(total, grad_out)
    save(rounded, grad_own_out)
    for copy in swaps:
        copy.wait_recv()
    links.finish()


def feed(n_dp, n_tensor, normed2, grad_rows, hidden1, gate_w, up_w, down_w, smalls):
    f32, bf16 = jnp.float32, jnp.bfloat16
    rows, width = hidden1.shape
    half = width // 2
    vmem = pl.BlockSpec(memory_space=pltpu.VMEM)
    hbm = pl.BlockSpec(memory_space=pl.ANY)
    weight = gate_w.shape
    inner = (GROUP, rows, n_tensor * weight[1])

    def shape(dims, dtype=bf16):
        return jax.ShapeDtypeStruct(tuple(dims), dtype)

    outs = [
        shape((rows, width), f32), shape((rows, width)), shape(normed2.shape),
        shape(weight), shape(weight), shape(weight), shape((n_tensor, weight[1], half)),
        shape((1, width), f32),
    ]
    scratch = [
        pltpu.VMEM(normed2.shape, bf16),
        pltpu.VMEM(normed2.shape, bf16),
        pltpu.VMEM(weight, bf16),
        pltpu.VMEM(weight, bf16),
        pltpu.VMEM(weight, bf16),
        pltpu.VMEM(inner, bf16),
        pltpu.VMEM(inner, bf16),
        pltpu.VMEM(inner, bf16),
        pltpu.VMEM(weight, bf16),
        pltpu.VMEM(weight, bf16),
        pltpu.VMEM(weight, bf16),
        pltpu.VMEM((2, rows, width), bf16),
        pltpu.VMEM((2, rows, width), bf16),
        pltpu.VMEM((rows, width), bf16),
        pltpu.VMEM((rows, width), bf16),
        pltpu.VMEM((rows, width), f32),
        pltpu.VMEM((rows, width), f32),
        pltpu.VMEM((rows, width), bf16),
        pltpu.VMEM((1, width), f32),
        pltpu.SemaphoreType.DMA((16,)),
        pltpu.SemaphoreType.DMA((16,)),
        pltpu.SemaphoreType.DMA((40,)),
    ]
    return pl.pallas_call(
        functools.partial(kernel_feed, n_dp, n_tensor),
        in_specs=[hbm] * 6 + [vmem],
        out_specs=[hbm] * len(outs),
        out_shape=outs,
        scratch_shapes=scratch,
        compiler_params=pltpu.CompilerParams(
            collective_id=2, has_side_effects=True, vmem_limit_bytes=67043328
        ),
        name="feed",
    )(normed2, grad_rows, hidden1, gate_w, up_w, down_w, smalls)


class Collect:
    def __init__(
        self, links, part, swapped, stage, arrived, late, blocks, target, mine, other, turned=False
    ):
        self.turned = turned
        self.links, self.part, self.swapped, self.stage = links, part, swapped, stage
        self.arrived, self.late, self.blocks, self.target = arrived, late, blocks, target
        self.mine, self.other = mine, other
        self.swaps, self.loads, self.deals = {}, [], []

    def issue(self, order):
        links = self.links
        for p in order:
            self.swaps[p] = links.send(
                self.part.at[p, :, self.other], self.swapped.at[p], bit=GROUP
            )
        if self.stage is not None:
            self.loads = [links.move(self.part.at[:, :, self.mine], self.stage)]

    def load(self, received):
        links = self.links
        self.loads = [
            links.move(self.part.at[:, :, self.mine], self.stage),
            links.move(received, self.swapped),
        ]

    def step(self, p):
        links, n, z = self.links, self.links.n_tensor, self.links.z_at
        f32, bf16 = jnp.float32, jnp.bfloat16
        while self.loads:
            self.loads.pop().wait()
        if p in self.swaps:
            self.swaps[p].wait_recv()
        own = self.stage[p] if self.stage is not None else self.part[p, :, self.mine]
        self.swapped[p] = (own.astype(f32) + self.swapped[p].astype(f32)).astype(bf16)
        if not hasattr(self, "ahead"):
            self.ahead, self.back, self.back_last = [None] * n, [None] * n, [None] * n
        source = self.swapped.at[p]
        self.ahead[p] = links.plan(
            source, self.arrived.at[p], shift=1, sends=z < p, receives=(z > 0) & (z <= p)
        )
        self.back[p] = links.plan(
            source, self.arrived.at[p], shift=-1, sends=z > p + 1,
            receives=(z > p) & (z < n - 1),
        )
        self.back_last[p] = links.plan(
            source, self.late, shift=-1, sends=z == p + 1, receives=(z == p) & (z < n - 1)
        )

        @pl.when((z == 0) & (z < p))
        def _():
            self.ahead[p].copy.start()

        @pl.when((z == n - 1) & (z > p + 1))
        def _():
            self.back[p].copy.start()

        @pl.when((z == n - 1) & (z == p + 1))
        def _():
            self.back_last[p].copy.start()

    def relay(self, i):
        links, n, z = self.links, self.links.n_tensor, self.links.z_at
        f32, bf16 = jnp.float32, jnp.bfloat16

        def add(p):
            self.swapped[p] = (
                self.swapped[p].astype(f32) + self.arrived[p].astype(f32)
            ).astype(bf16)

        for p in range(n):
            at = i - (n - 1) + p
            if 0 < at < n - 1 and at < p:

                @pl.when(z == at)
                def _(p=p):
                    self.ahead[p].copy.wait_recv()
                    add(p)
                    self.ahead[p].copy.start()

            at = n - 1 - i + p
            if 0 < at < n - 1 and at > p:

                @pl.when(z == at)
                def _(p=p, at=at):
                    self.back[p].copy.wait_recv()
                    add(p)
                    (self.back_last if at == p + 1 else self.back)[p].copy.start()

    def finish(self):
        links, n, z = self.links, self.links.n_tensor, self.links.z_at
        f32, bf16 = jnp.float32, jnp.bfloat16
        member = links.d_at % GROUP
        for p in range(n):

            @pl.when((z == p) & (z > 0))
            def _(p=p):
                self.ahead[p].copy.wait_recv()

            @pl.when((z == p) & (z < n - 1))
            def _(p=p):
                self.back_last[p].copy.wait_recv()

        below = jnp.where(z > 0, self.arrived[z].astype(f32), 0.0)
        above = jnp.where(z < n - 1, self.late[...].astype(f32), 0.0)
        total = (self.swapped[z].astype(f32) + below + above).astype(bf16)
        chunk = total.shape[1] // GROUP
        size = self.blocks.shape[2 if self.turned else 1]
        place = pl.ds(pl.multiple_of(member * size, 16), size)
        if self.turned:
            place = pl.ds(pl.multiple_of(member * size, TILE), size)
        for i in range(GROUP):
            block = total[:, i * chunk : (i + 1) * chunk]
            self.blocks[i] = block.T if self.turned else block
        if self.turned:
            target = self.target.at[:, place]
        elif len(self.target.shape) == 2:
            target = self.target.at[place, :]
        else:
            target = self.target.at[member]
        for k in range(1, GROUP):
            self.deals.append(links.send(self.blocks.at[member ^ k], target, bit=k))
        links.save(self.blocks.at[member], target)

    def wait(self):
        for deal in self.deals:
            deal.wait_recv()


def kernel_backward(
    n_dp, n_tensor,
    grad_own, hidden_grad, tokens, hidden1, mlp_part, n1_in, query_in, keyval_in, log_in, att_in,
    cos_in, sin_in, qkv_in, out_in, small_in, down_in, gate_in, up_in, down_got,
    mlp_row, fixed,
    input_out, block_out, qkv_out, out_out, gate_out, up_out, down_out,
    g_all, n1_all, qkv, outw, queries, keyvals, logs, att, cosine, sine, gains, low_col,
    att_grad, other_grad, totals, query_total, pass_on, delta, halo_send, halo_recv,
    to_core, from_core, to_across, from_across, mlp_across, hidden, stage, gate_stage,
    down_swap, gate_swap, up_swap, out_swap, qkv_swap,
    down_come, gate_come, up_come, out_come, qkv_come,
    down_late, gate_late, up_late, out_late, qkv_late,
    down_block, gate_block, up_block, out_block, qkv_block,
    out_sems, in_sems, local_sems,
):
    f32, bf16 = jnp.float32, jnp.bfloat16
    links = Links(n_dp, n_tensor, out_sems, in_sems, local_sems)
    send, move, save = links.send, links.move, links.save
    d_at, z_at = links.d_at, links.z_at
    core = d_at % 2
    upper = d_at // GROUP
    rows, width = grad_own.shape
    half = width // 2
    contract = (((1,), (1,)), ((), ()))
    over_rows = (((0,), (0,)), ((), ()))
    mine = pl.ds(pl.multiple_of(upper * half, half), half)
    other = pl.ds(pl.multiple_of((1 - upper) * half, half), half)
    tiles = rows // TILE
    span = TILE + WINDOW
    quarter = qkv.shape[1]
    out_quarter = outw.shape[1]
    extra = qkv_swap.shape[1] - quarter

    loads = [
        move(grad_own, g_all.at[0]), move(out_in, outw), move(query_in, queries),
        move(keyval_in, keyvals), move(log_in, logs), move(cos_in, cosine), move(sin_in, sine),
        move(mlp_part.at[pl.ds(0, 2)], to_core), move(hidden1, hidden), move(att_in, att),
        move(qkv_in, qkv), move(n1_in, n1_all),
    ]
    small = pltpu.make_async_copy(small_in, gains, local_sems.at[links.used_local])
    links.used_local += 1
    small.start()
    links.barrier()
    across = send(grad_own, g_all.at[1], bit=2)
    beside = send(grad_own, g_all.at[2], bit=1)
    mlp_core = send(mlp_part.at[pl.ds(2, 2)], from_core, bit=1)
    order = []
    for i in range((n_tensor + 1) // 2):
        order.extend(dict.fromkeys((n_tensor - 1 - i, i)))

    down = Collect(
        links, down_in, down_swap, stage, down_come, down_late, down_block, down_out, mine, other
    )
    gate = Collect(
        links, gate_in, gate_swap, gate_stage, gate_come, gate_late, gate_block, gate_out, mine, other,
        turned=True,
    )
    up = Collect(
        links, up_in, up_swap, stage, up_come, up_late, up_block, up_out, mine, other, turned=True
    )
    out_part = g_all.at[:, pl.ds(quarter + extra, out_quarter), :]
    qkv_part = g_all.at[:, pl.ds(0, quarter + extra), :]
    out_collect = Collect(
        links, out_part, out_swap, None, out_come, out_late, out_block, out_out, mine, other
    )
    qkv_collect = Collect(
        links, qkv_part, qkv_swap, None, qkv_come, qkv_late, qkv_block, qkv_out, mine, other
    )
    down.load(down_got)
    gate.issue(order)
    small.wait()
    for m, k in ((0, 0), (1, 2)):
        info = gains[d_at ^ k].T
        low_col[m] = info[:, 1:2].astype(jnp.int32) - z_at * rows + WINDOW
    loads[0].wait()
    loads[1].wait()

    def attended_back(b):
        units = outw.shape[0] * outw.shape[1]
        att_grad[b] = lax.dot_general(
            g_all[b], outw[...].reshape(units, width), contract, preferred_element_type=f32
        ).astype(bf16)

    attended_back(0)
    beside.wait_recv()
    attended_back(2)
    grad_swap = send(att_grad.at[2], other_grad.at[0], bit=1)
    for p in order:
        down.step(p)
    up.issue(order)
    for copy in loads[2:]:
        copy.wait()
    mlp_core.wait_recv()
    heads = queries.shape[2] // HEAD_SIZE
    repeat = QUERY_HEADS // KEY_VALUE_HEADS
    scale = HEAD_SIZE ** (-0.5)
    is_first = core == 0
    second, keys_turn, all_turn = fixed[1:2], fixed[2:3], fixed[3:4]

    def back_tile(m, tile):
        start = tile * TILE
        at = slice(start, start + TILE)
        reach = slice(start, start + span)
        key = lax.broadcasted_iota(jnp.int32, (TILE, span), 1)
        query = lax.broadcasted_iota(jnp.int32, (TILE, span), 0)
        allowed = (key >= low_col[m, at, :] - start) & (key <= query + WINDOW)
        own, others = att_grad[m, at, :], other_grad[m, at, :]
        by_repeat = (jnp.where(is_first, own, others), jnp.where(is_first, others, own))
        for group in range(heads // repeat):
            base = group * 2 * HEAD_SIZE
            k = keyvals[m, reach, base : base + HEAD_SIZE]
            v = keyvals[m, reach, base + HEAD_SIZE : base + 2 * HEAD_SIZE]
            key_sum = None
            for r in range(repeat):
                head = group * repeat + r
                q = queries[m, at, head * HEAD_SIZE : (head + 1) * HEAD_SIZE]
                g = by_repeat[r][:, group * HEAD_SIZE : (group + 1) * HEAD_SIZE]
                s = lax.dot_general(q, k, contract, preferred_element_type=f32) * scale
                total = logs[m, at, head : head + 1]
                p = jnp.exp(jnp.where(allowed, s, NEG_FILL) - total)
                pg = lax.dot_general(g, v, contract, preferred_element_type=f32)
                inner = jnp.sum(p * pg, axis=1, keepdims=True)
                sg = (p * (pg - inner) * scale).astype(bf16)
                query_total[:, head * HEAD_SIZE : (head + 1) * HEAD_SIZE] = jnp.dot(
                    sg, k, preferred_element_type=f32
                )
                dk = lax.dot_general(sg, q, over_rows, preferred_element_type=f32)
                dv = lax.dot_general(p.astype(bf16), g, over_rows, preferred_element_type=f32)
                both = jnp.concatenate([dk, dv], axis=1)
                key_sum = both if key_sum is None else key_sum + both
            totals[m, reach, base : base + 2 * HEAD_SIZE] += key_sum
        turned = turn(
            query_total[...], cosine[m, at, :], sine[m, at, :], second, all_turn, -1.0
        ).astype(bf16)

        @pl.when(is_first)
        def _():
            delta[m, at, :] = turned

        @pl.when(core != 0)
        def _():
            pass_on[m, at, :] = turned

    halos = [
        links.plan(
            halo_send.at[m], halo_recv.at[m], shift=-1, sends=z_at > 0,
            receives=z_at < n_tensor - 1,
        )
        for m in range(2)
    ]

    def send_halo(m):
        halo_send[m] = totals[m, :WINDOW].astype(bf16)
        halos[m].start()

    def finish_block(m):
        halos[m].wait_recv()
        full = totals[m, WINDOW:]
        tail = full[rows - WINDOW :] + jnp.where(
            z_at < n_tensor - 1, halo_recv[m].astype(f32), 0.0
        )
        full = jnp.concatenate([full[: rows - WINDOW], tail], axis=0)
        turned = turn(full, cosine[m], sine[m], second, keys_turn, -1.0).astype(bf16)

        @pl.when(is_first)
        def _():
            pass_on[m] = turned

        @pl.when(core != 0)
        def _():
            delta[m] = turned

        return send(pass_on.at[m], delta.at[2 + m], bit=1)

    first_steps = n_tensor // 2
    free = -(-WINDOW // TILE)
    totals[...] = jnp.zeros_like(totals)
    grad_swap.wait_recv()
    for tile in range(free):
        back_tile(0, tile)
    send_halo(0)
    down.relay(1)
    gate.step(order[0])
    for tile in range(free, tiles):
        back_tile(0, tile)
    for p in order[1:first_steps]:
        gate.step(p)
    for i in range(2, n_tensor - 1):
        down.relay(i)
    across.wait_recv()
    both = send(g_all.at[1], g_all.at[3], bit=1)
    to_across[...] = (to_core[1].astype(f32) + from_core[1].astype(f32)).astype(bf16)
    mlp_send = send(to_across, mlp_across, bit=2)
    hidden[...] += to_core[0].astype(f32) + from_core[0].astype(f32)
    attended_back(1)
    both.wait_recv()
    attended_back(3)
    grad_swap = send(att_grad.at[3], other_grad.at[1], bit=1)

    def weight_grad(left, right, at):
        total = None
        for b in range(GROUP):
            term = lax.dot_general(
                left[b, :, at], right[b], over_rows, preferred_element_type=f32
            )
            total = term if total is None else total + term
        return total

    out_grad = weight_grad(att, g_all, slice(0, n_tensor * out_quarter)).astype(bf16)
    both.wait_send()
    links.sent.remove(both)
    out_part[...] = out_grad.reshape(n_tensor, out_quarter, width)
    grad_swap.wait_recv()
    back_tile(1, 0)
    down.finish()
    for tile in range(1, free):
        back_tile(1, tile)
    send_halo(1)
    for p in order[first_steps:]:
        gate.step(p)
    for tile in range(free, tiles):
        back_tile(1, tile)
    swap0 = finish_block(0)
    gate.relay(1)
    up.step(order[0])
    swap1 = finish_block(1)

    def project_back(b):
        units = qkv.shape[0] * quarter
        return jnp.dot(delta[b], qkv[...].reshape(units, width), preferred_element_type=f32)

    mlp_send.wait_recv()
    mlp_across[...] = (hidden[...] + mlp_across[...].astype(f32)).astype(bf16)
    save(mlp_across, block_out)
    mlp_send.wait_send()
    links.sent.remove(mlp_send)
    swap1.wait_recv()
    to_core[1] = project_back(3).astype(bf16)
    core_send1 = send(to_core.at[1], from_core.at[1], bit=1)
    hidden[...] = project_back(1)
    swap0.wait_recv()
    to_core[0] = project_back(2).astype(bf16)
    core_send0 = send(to_core.at[0], from_core.at[0], bit=1)
    core_send1.wait_recv()
    across_sends = []
    for i in range(tiles):
        at = pl.ds(i * TILE, TILE)
        to_across[at] = (hidden[at, :] + from_core[1, at, :].astype(f32)).astype(bf16)
        across_sends.append(send(to_across.at[at], from_across.at[at], bit=2))
    hidden[...] = project_back(0)
    core_send0.wait_recv()
    hidden[...] += from_core[0].astype(f32)
    for p in order[1 : n_tensor - 1]:
        up.step(p)
    attn_row = None
    for p in range(n_tensor):
        at = slice(p * quarter, (p + 1) * quarter)
        grad = weight_grad(delta, n1_all, at)
        row = jnp.sum(grad * qkv[p].astype(f32), axis=0, keepdims=True)
        attn_row = row if attn_row is None else attn_row + row
        qkv_part[p, :quarter, :] = grad.astype(bf16)
    ending = jnp.concatenate(
        [attn_row, mlp_row[...], jnp.zeros((extra - 2, width), f32)], axis=0
    ).astype(bf16)
    for p in range(n_tensor):
        qkv_part[p, quarter:, :] = ending
    qkv_collect.issue(order)
    out_collect.issue(order)
    finals = [
        move(tokens, n1_all.at[0]),
        move(hidden_grad.at[:, pl.ds(0, half)], totals.at[0, pl.ds(0, rows)]),
        move(hidden_grad.at[:, pl.ds(half, half)], totals.at[1, pl.ds(0, rows)]),
    ]
    for p in order[n_tensor - 1 :]:
        up.step(p)
    for i in range(2, n_tensor - 1):
        gate.relay(i)
    gain = jnp.concatenate([gains[i, 2:3, : width // n_dp] for i in range(n_dp)], axis=1)
    for copy in finals:
        copy.wait()
    for i in range(tiles):
        at = pl.ds(i * TILE, TILE)
        across_sends[i].wait_recv()
        upstream = hidden[at, :] + from_across[at, :].astype(f32)
        features = n1_all[0, at, :].astype(f32)
        inverse = lax.rsqrt(jnp.mean(features * features, axis=1, keepdims=True) + EPS)
        scaled = gain * upstream
        mean = jnp.mean(scaled * features, axis=1, keepdims=True)
        change = inverse * scaled - features * (inverse * inverse * inverse) * mean
        n1_all[1, at, :half] = (totals[0, at, :] + change[:, :half]).astype(bf16)
        n1_all[1, at, half:] = (totals[1, at, :] + change[:, half:]).astype(bf16)
        if i == 1:
            up.relay(1)
    save(n1_all.at[1], input_out)
    gate.finish()
    for p in order[: n_tensor - 1]:
        qkv_collect.step(p)
    for i in range(2, n_tensor - 1):
        up.relay(i)
    for p in order[n_tensor - 1 :]:
        qkv_collect.step(p)
    qkv_collect.relay(1)
    up.finish()
    for p in order:
        out_collect.step(p)
    for i in range(2, n_tensor - 1):
        qkv_collect.relay(i)
    out_collect.relay(1)
    qkv_collect.finish()
    for i in range(2, n_tensor - 1):
        out_collect.relay(i)
    out_collect.finish()
    for collect in (down, gate, up, out_collect, qkv_collect):
        collect.wait()
    links.finish()


def backward(
    n_dp, n_tensor, grad_own, hidden_grad, tokens, hidden1, mlp_part, normed1, queries, keyvals, logs, attended,
    cosine, sine, qkv_full, out_full, smalls, down_part, gate_part, up_part, down_got,
    mlp_row, fixed,
):
    f32, bf16 = jnp.float32, jnp.bfloat16
    rows, width = grad_own.shape
    half = width // 2
    chunk = width // n_dp
    units = queries.shape[2]
    vmem = pl.BlockSpec(memory_space=pltpu.VMEM)
    hbm = pl.BlockSpec(memory_space=pl.ANY)
    extra = 16
    quarters = [
        down_part.shape[1], gate_part.shape[1], up_part.shape[1], out_full.shape[1],
        qkv_full.shape[1] + extra,
    ]

    def shape(dims, dtype=bf16):
        return jax.ShapeDtypeStruct(tuple(dims), dtype)

    def finals(index):
        return shape((GROUP, quarters[index], chunk))

    outs = [
        shape((rows, width)), shape((rows, width)), finals(4), shape((GROUP * quarters[3], chunk)),
        shape((chunk, GROUP * quarters[1])), shape((chunk, GROUP * quarters[2])),
        shape((GROUP * quarters[0], chunk)),
    ]
    full = (GROUP, rows, width)
    scratch = [
        pltpu.VMEM(full, bf16),
        pltpu.VMEM(full, bf16),
        pltpu.VMEM(qkv_full.shape, bf16),
        pltpu.VMEM(out_full.shape, bf16),
        pltpu.VMEM(queries.shape, bf16),
        pltpu.VMEM(keyvals.shape, bf16),
        pltpu.VMEM(logs.shape, f32),
        pltpu.VMEM(attended.shape, bf16),
        pltpu.VMEM(cosine.shape, f32),
        pltpu.VMEM(sine.shape, f32),
        pltpu.VMEM(smalls.shape, f32),
        pltpu.VMEM((2, rows, 1), jnp.int32),
        pltpu.VMEM(attended.shape, bf16),
        pltpu.VMEM((2,) + attended.shape[1:], bf16),
        pltpu.VMEM((2, rows + WINDOW, units), f32),
        pltpu.VMEM((TILE, units), f32),
        pltpu.VMEM((2, rows, units), bf16),
        pltpu.VMEM((GROUP, rows, units), bf16),
        pltpu.VMEM((2, WINDOW, units), bf16),
        pltpu.VMEM((2, WINDOW, units), bf16),
        pltpu.VMEM((2, rows, width), bf16),
        pltpu.VMEM((2, rows, width), bf16),
        pltpu.VMEM((rows, width), bf16),
        pltpu.VMEM((rows, width), bf16),
        pltpu.VMEM((rows, width), bf16),
        pltpu.VMEM((rows, width), f32),
        pltpu.VMEM((n_tensor, quarters[0], half), bf16),
        pltpu.VMEM((n_tensor, quarters[1], half), bf16),
    ]
    scratch += [pltpu.VMEM((n_tensor, q, half), bf16) for q in quarters]
    scratch += [pltpu.VMEM((n_tensor, q, half), bf16) for q in quarters]
    scratch += [pltpu.VMEM((q, half), bf16) for q in quarters]
    scratch += [
        pltpu.VMEM((GROUP, chunk, q) if turned else (GROUP, q, chunk), bf16)
        for q, turned in zip(quarters, (False, True, True, False, False))
    ]
    scratch += [
        pltpu.SemaphoreType.DMA((160,)),
        pltpu.SemaphoreType.DMA((160,)),
        pltpu.SemaphoreType.DMA((40,)),
    ]
    return pl.pallas_call(
        functools.partial(kernel_backward, n_dp, n_tensor),
        in_specs=[hbm] * 19 + [vmem] * 2,
        out_specs=[hbm] * len(outs),
        out_shape=outs,
        scratch_shapes=scratch,
        compiler_params=pltpu.CompilerParams(
            collective_id=1, has_side_effects=True, vmem_limit_bytes=67043328
        ),
        name="backward",
    )(
        grad_own, hidden_grad, tokens, hidden1, mlp_part, normed1, queries, keyvals, logs, attended, cosine, sine,
        qkv_full, out_full, smalls, down_part, gate_part, up_part, down_got, mlp_row, fixed,
    )


def fast_local(
    n_dp,
    n_tensor,
    block_in,
    cotangent,
    segment_ids,
    attn_gain,
    qkv_weight,
    out_weight,
    mlp_gain,
    gate_weight,
    up_weight,
    down_weight,
):
    bf16, f32 = jnp.bfloat16, jnp.float32
    rows, width = block_in.shape
    part = attn_gain.shape[0]
    (
        normed1, normed2, hidden1, queries, keyvals, log_total, attended, cosine, sine, qkv_full,
        out_full, smalls, grad_rows, gate_full, up_full, down_full,
    ), fixed = forward(
        n_dp, n_tensor, block_in, cotangent, segment_ids, jnp.stack([attn_gain, mlp_gain]),
        qkv_weight, out_weight, gate_weight, up_weight, down_weight,
    )
    (
        hidden1_grad, grad_own, mlp_part, down_part, gate_part, up_part, down_got, mlp_row,
    ) = feed(n_dp, n_tensor, normed2, grad_rows, hidden1, gate_full, up_full, down_full, smalls)
    input_grad, block_out, qkv_blocks, out_grad, gate_grad, up_grad, down_grad = backward(
        n_dp, n_tensor, grad_own, hidden1_grad, block_in, hidden1, mlp_part, normed1, queries,
        keyvals, log_total, attended, cosine, sine, qkv_full, out_full, smalls, down_part, gate_part, up_part, down_got, mlp_row,
        fixed,
    )
    quarter = qkv_full.shape[1]

    def row_of(index, gain):
        return jnp.sum(qkv_blocks[:, quarter + index].astype(f32), axis=0) / gain.astype(f32)

    blocks = qkv_blocks[:, :quarter]
    qkv_grad = blocks.reshape(-1, blocks.shape[2]).T.astype(f32)
    gains = [row_of(0, attn_gain), row_of(1, mlp_gain)]
    return (
        block_out,
        input_grad,
        gains[0],
        qkv_grad,
        out_grad.astype(f32),
        gains[1],
        gate_grad.astype(f32),
        up_grad.astype(f32),
        down_grad.astype(f32),
    )


def solution(mesh):
    in_specs = (
        P(("dp", "tensor"), None),
        P(("dp", "tensor"), None),
        P("dp", None),
        P("dp"),
        P("dp", "tensor"),
        P("tensor", "dp"),
        P("dp"),
        P("dp", "tensor"),
        P("dp", "tensor"),
        P("tensor", "dp"),
    )
    out_specs = (
        P(("dp", "tensor"), None),
        P(("dp", "tensor"), None),
        P("dp"),
        P("dp", "tensor"),
        P("tensor", "dp"),
        P("dp"),
        P("dp", "tensor"),
        P("dp", "tensor"),
        P("tensor", "dp"),
    )
    n_dp, n_tensor = mesh.shape["dp"], mesh.shape["tensor"]

    def body(*arrays):
        rows = arrays[0].shape[0]
        groups = arrays[4].shape[1] // (4 * HEAD_SIZE)
        if n_dp == 2 * GROUP and groups == 2 and rows >= WINDOW and rows % TILE == 0:
            return fast_local(n_dp, n_tensor, *arrays)
        return local(*arrays)

    return jax.shard_map(body, mesh=mesh, in_specs=in_specs, out_specs=out_specs, check_vma=False)
```

profile of v0, /device:TPU:0, one launch (start us, length us, event | category | flops | bytes accessed | tf_op | source)
XLA Modules:
  0.0 413.7 jit_solution(1651807118061327031)
XLA Ops:
  0.6 0.7 stack.9
  1.3 0.7 stack.10
  2.0 0.6 pad_maximum_fusion.gain_rows
  2.5 1.7 copy.20.out_w
  4.3 2.0 copy.21.down_w
  6.3 164.7 %forward.1 = (bf16[4,384,1536]{2,1,0:T(8,128)(2,1)}, bf16[4,384,1536]{2,1,0:T(8,128)(2,1)}, f32[384,1536]{1,0:T(8,128)}, bf16[2,384,768]{2,1,0:T(8,128)(2,1)}, b...) custom-call(bf16[384,1536]{1,0:T(8,128)(2,1)} %tokens.3, ...), custom_call_target="tpu_custom_call" | custom-call | tf_op jit(solution)/shard_map/forward/pallas_call | solution.py:795
  171.0 80.0 %feed.1 = (f32[384,1536]{1,0:T(8,128)}, bf16[384,1536]{1,0:T(8,128)(2,1)}, bf16[4,384,1536]{2,1,0:T(8,128)(2,1)}, bf16[4,256,1536]{2,1,0:T(8,128)(2,1)}, bf16[4,...) custom-call(bf16[4,384,1536]{2,1,0:T(8,128)(2,1)} %get-tuple-element.4, ...), custom_call_target="tpu_custom_call" | custom-call | tf_op jit(solution)/shard_map/feed/pallas_call | solution.py:987
  251.0 151.2 %backward.1 = (bf16[384,1536]{1,0:T(8,128)(2,1)}, bf16[384,1536]{1,0:T(8,128)(2,1)}, bf16[4,208,192]{2,1,0:T(8,128)(2,1)}, bf16[384,192]{1,0:T(8,128)(2,1)}, bf1...) custom-call(bf16[384,1536]{1,0:T(8,128)(2,1)} %get-tuple-element.47.grad_own, ...), custom_call_target="tpu_custom_call" | custom-call | tf_op jit(solution)/shard_map/backward/pallas_call | solution.py:1518
  402.2 0.0 copy-start.4
  402.2 0.8 convert_reduce_fusion
  403.0 1.0 slice.10
  404.0 1.2 convert_divide_fusion
  405.3 1.8 copy.23
  407.0 0.0 copy-start.3
  407.0 0.1 bitcast_convert_fusion
  407.1 0.0 copy-start.2
  407.1 1.1 copy.22
  408.2 0.0 copy-start.1
  408.2 0.0 copy-done.4
  408.2 1.0 convert_element_type.43
  409.2 0.0 copy-done.3
  409.2 1.0 convert_element_type.44
  410.1 0.0 copy-done.2
  410.1 0.0 copy-start
  410.1 1.1 copy.24
  411.2 0.0 copy-done.1
  411.2 1.0 copy.27
  412.2 0.0 copy-done
  412.2 1.0 copy.28
Async XLA Ops:
  402.2 6.0 %copy-start.4 = (bf16[192,1024]{1,0:T(8,128)(2,1)S(1)}, bf16[192,1024]{1,0:T(8,128)(2,1)}, u32[]{:S(2)}) copy-start(bf16[192,1024]{1,0:T(8,128)(2,1)} %get-tuple-element.68) | copy-start | bytes 1179652
  407.0 2.1 copy-start.3
  407.1 3.0 copy-start.2
  408.2 3.0 copy-start.1
  410.1 2.1 copy-start
where the time goes:
time: 417 us; the launch traced here: 414 us
  Pallas kernels  396 us (95%)
  local copies, waits for them, and re-layouts  12 us (3%)
  other arithmetic  4.65 us (1%)
    pallas_call x1, Pallas kernels, forward(): pl.pallas_call(functools.partial(kernel_forward, n_dp, n_tensor), in_spec...  165 us
    pallas_call x1, Pallas kernels, backward(): pl.pallas_call(functools.partial(kernel_backward, n_dp, n_tensor), in_spe...  151 us
    pallas_call x1, Pallas kernels, feed(): pl.pallas_call(functools.partial(kernel_feed, n_dp, n_tensor), in_specs=[...  80 us
    unnamed x16, local copies, waits for them, and re-layouts  8.59 us

commit v1 on v0

--- a/solution.py
+++ b/solution.py
@@ -397,10 +397,10 @@
 
 def kernel_forward(
     n_dp, n_tensor,
-    tokens, cot, out_w, gate_w, up_w, down_w, qkv_w, segments, gain_rows, fixed,
+    tokens, cot, gate_w, up_w, down_w, out_w, qkv_w, segments, gain_rows, fixed,
     normed1_out, normed2_out, hidden_out, query_out, keyval_out, log_out, att_out,
     cos_out, sin_out, qkv_out, out_out, small_out, cot_out, gate_out, up_out, down_out,
-    x_all, n1_all, first, dealt, first_piece, qkv, obuf, gbuf, ubuf, dbuf, piece, outw,
+    x_all, n1_all, first, dealt, first_piece, qkv, out_parcel, obuf, gbuf, ubuf, dbuf, piece, outw,
     small, small_all, stream, parts, recv, queries, keyvals,
     att, by_repeat, logs, cosine, sine, low_col, to_core, from_core, to_across, from_across,
     hidden, n2_all, stage, out_sems, in_sems, local_sems,
@@ -422,6 +422,10 @@
     quarter = turned.shape[0] // GROUP
     for i in range(GROUP):
         first[i] = turned[i * quarter : (i + 1) * quarter]
+    turned = out_w[...].T
+    out_quarter = turned.shape[0] // GROUP
+    for i in range(GROUP):
+        out_parcel[i] = turned[i * out_quarter : (i + 1) * out_quarter]
     ids = segments[...]
     seqs, length = ids.shape
     begin = jnp.zeros_like(ids)
@@ -448,21 +452,28 @@
     deals = [send(first.at[member ^ k], dealt.at[member], bit=k) for k in range(1, GROUP)]
     beside = send(tokens, x_all.at[2], bit=1)
     smalls = [send(small, small_all.at[d_at], bit=k) for k in range(1, n_dp)]
-    rests = []
-
-    def rows_of(ref, at):
-        size = ref.shape[0] // GROUP
-        return ref.at[pl.ds(pl.multiple_of(at * size, 16), size), :]
-
     def columns_of(ref, at):
         size = ref.shape[1] // GROUP
         return ref.at[:, pl.ds(pl.multiple_of(at * size, TILE), size)]
 
-    pairs = [(out_w, obuf, rows_of), (gate_w, gbuf, columns_of), (up_w, ubuf, columns_of)]
-    pairs.append((down_w, dbuf, rows_of))
-    for ref, buffer, take in pairs:
-        for k in range(1, GROUP):
-            rests.append(send(take(ref, member ^ k), buffer.at[member], bit=k))
+    def parcel_of(ref, at):
+        return ref.at[at]
+
+    pairs = [
+        (out_parcel, obuf, parcel_of), (gate_w, gbuf, columns_of), (up_w, ubuf, columns_of),
+        (down_w, dbuf, columns_of),
+    ]
+
+    def deal(group):
+        return [
+            send(take(ref, member ^ k), buffer.at[member], bit=k)
+            for ref, buffer, take in group
+            for k in range(1, GROUP)
+        ]
+
+    rests = deal(pairs[:2])
+    across = send(tokens, x_all.at[1], bit=2)
+    late_rests = deal(pairs[2:])
     own = [move(tokens, x_all.at[0])]
     for ref, buffer, take in pairs:
         own.append(move(take(ref, member), buffer.at[member]))
@@ -507,23 +518,20 @@
         )
     for copy in rests:
         copy.wait_recv()
-    across = send(tokens, x_all.at[1], bit=2)
-    sizes = [obuf.shape[1], gbuf.shape[2], ubuf.shape[2], dbuf.shape[1]]
+    sizes = [obuf.shape[1], gbuf.shape[2], ubuf.shape[2], dbuf.shape[2]]
     starts = [sum(sizes[:i]) for i in range(len(sizes))]
-    spreads = []
-    for index, (target, buffer) in enumerate(
-        ((outw, obuf), (gate_out, gbuf), (up_out, ubuf), (down_out, dbuf))
-    ):
+    saves = []
+
+    def prepare(index, target, buffer):
         at = slice(starts[index], starts[index] + sizes[index])
         for i in range(GROUP):
-            value = buffer[i]
-            piece[at, i * chunk : (i + 1) * chunk] = (
-                value.T if value.shape[0] == chunk and sizes[index] != chunk else value
-            )
+            piece[at, i * chunk : (i + 1) * chunk] = buffer[i] if index == 0 else buffer[i].T
         own_piece = piece.at[pl.ds(starts[index], sizes[index])]
-        spreads.append(Spread(links, own_piece, target, columns))
-    out_spread, gate_spread, up_spread, down_spread = spreads
-    saves = [move(s.own_piece, s.target.at[z_at, :, columns]) for s in spreads]
+        saves.append(move(own_piece, target.at[z_at, :, columns]))
+        return Spread(links, own_piece, target, columns)
+
+    out_spread = prepare(0, outw, obuf)
+    gate_spread = prepare(1, gate_out, gbuf)
     out_spread.issue()
     spread_first.step(3)
     gate_spread.issue()
@@ -593,6 +601,11 @@
     save(sine, sin_out)
     take_block(1, part_swap)
     gate_spread.step(1)
+    for copy in late_rests:
+        copy.wait_recv()
+    up_spread = prepare(2, up_out, ubuf)
+    down_spread = prepare(3, down_out, dbuf)
+    up_spread.issue()
     save(queries, query_out)
     heads = queries.shape[2] // HEAD_SIZE
     repeat = QUERY_HEADS // KEY_VALUE_HEADS
@@ -624,19 +637,16 @@
     for tile in range(free, tiles):
         attend_tile(1, tile * TILE)
         attend_tile(0, tile * TILE)
-    gate_spread.step(2)
     halos[0].wait_recv()
     halos[1].wait_recv()
-    up_spread.issue()
     for tile in range(free):
         attend_tile(1, tile * TILE)
     att_swap1 = send(by_repeat.at[1 - core, 1], att.at[3], bit=1)
-    gate_spread.step(3)
-    attend_tile(0, 0)
-    up_spread.step(1)
-    for tile in range(1, free):
+    gate_spread.step(2)
+    for tile in range(free):
         attend_tile(0, tile * TILE)
     att_swap0 = send(by_repeat.at[1 - core, 0], att.at[2], bit=1)
+    gate_spread.step(3)
     save(keyvals, keyval_out)
     save(logs, log_out)
     att[0] = by_repeat[core, 0]
@@ -669,8 +679,10 @@
     core_send0.wait_recv()
     hidden[...] += from_core[0].astype(f32)
     save(att, att_out)
-    up_spread.step(2)
-    steps = [(up_spread, 3), (down_spread, 1), (down_spread, 2), (down_spread, 3)]
+    up_spread.step(1)
+    steps = [
+        (up_spread, 2), (up_spread, 3), (down_spread, 1), (down_spread, 2), (down_spread, 3),
+    ]
     last = []
     for i in range(tiles):
         at = pl.ds(i * TILE, TILE)
@@ -681,7 +693,7 @@
         n2_all[0, at, :] = (value * scale * gains[1]).astype(bf16)
         last.append(send(n2_all.at[0, at], n2_all.at[1, at], bit=2))
         last.append(send(n2_all.at[0, at], n2_all.at[2, at], bit=1))
-        if i in (1, 2):
+        if i < 3:
             spread, s = steps.pop(0)
             spread.step(s)
     save(hidden, hidden_out)
@@ -711,6 +723,7 @@
 def forward(
     n_dp, n_tensor, tokens, cot, segments, gain_rows, qkv_w, out_w, gate_w, up_w, down_w
 ):
+    out_w, down_w = out_w.T, down_w.T
     rows, width = tokens.shape
     f32, bf16 = jnp.float32, jnp.bfloat16
     vmem = pl.BlockSpec(memory_space=pltpu.VMEM)
@@ -718,8 +731,8 @@
     chunk = qkv_w.shape[0]
     quarter = qkv_w.shape[1] // GROUP
     sizes = [
-        out_w.shape[0] // GROUP, gate_w.shape[1] // GROUP, up_w.shape[1] // GROUP,
-        down_w.shape[0] // GROUP,
+        out_w.shape[1] // GROUP, gate_w.shape[1] // GROUP, up_w.shape[1] // GROUP,
+        down_w.shape[1] // GROUP,
     ]
     units = quarter * n_tensor
     heads = units // HEAD_SIZE
@@ -763,9 +776,10 @@
         pltpu.VMEM((quarter, width // 2), bf16),
         pltpu.VMEM(qkv_shape, bf16),
         pltpu.VMEM((GROUP, sizes[0], chunk), bf16),
+        pltpu.VMEM((GROUP, sizes[0], chunk), bf16),
         pltpu.VMEM((GROUP, chunk, sizes[1]), bf16),
         pltpu.VMEM((GROUP, chunk, sizes[2]), bf16),
-        pltpu.VMEM((GROUP, sizes[3], chunk), bf16),
+        pltpu.VMEM((GROUP, chunk, sizes[3]), bf16),
         pltpu.VMEM((sum(sizes), width // 2), bf16),
         pltpu.VMEM(out_shape, bf16),
         pltpu.VMEM((8, rows), f32),
@@ -794,7 +808,7 @@
     ]
     results = pl.pallas_call(
         functools.partial(kernel_forward, n_dp, n_tensor),
-        in_specs=[hbm] * 6 + [vmem] * 4,
+        in_specs=[hbm] * 5 + [vmem] * 5,
         out_specs=[hbm] * len(outs),
         out_shape=outs,
         scratch_shapes=scratch,
@@ -803,7 +817,7 @@
         ),
         name="forward",
     )(
-        tokens, cot, out_w, gate_w, up_w, down_w, qkv_w, segments, gain_rows, jnp.asarray(fixed)
+        tokens, cot, gate_w, up_w, down_w, out_w, qkv_w, segments, gain_rows, jnp.asarray(fixed)
     )
     return results, jnp.asarray(fixed)
 
@@ -904,7 +918,7 @@
             part[p] = grad.astype(bf16)
             if weight is not None:
                 row[...] += jnp.sum(grad * weight[p].astype(f32), axis=0, keepdims=True)
-            else:
+            elif p in order[: n_tensor // 2]:
                 swaps.append(send(part.at[p, :, other], down_got.at[p], bit=GROUP))
             save(part.at[p], target.at[p])
 
@@ -1016,12 +1030,11 @@
         if self.stage is not None:
             self.loads = [links.move(self.part.at[:, :, self.mine], self.stage)]
 
-    def load(self, received):
+    def load(self, received, order):
         links = self.links
-        self.loads = [
-            links.move(self.part.at[:, :, self.mine], self.stage),
-            links.move(received, self.swapped),
-        ]
+        count = links.n_tensor // 2
+        self.issue(order[count:])
+        self.loads += [links.move(received.at[p], self.swapped.at[p]) for p in order[:count]]
 
     def step(self, p):
         links, n, z = self.links, self.links.n_tensor, self.links.z_at
@@ -1177,7 +1190,8 @@
         order.extend(dict.fromkeys((n_tensor - 1 - i, i)))
 
     down = Collect(
-        links, down_in, down_swap, stage, down_come, down_late, down_block, down_out, mine, other
+        links, down_in, down_swap, stage, down_come, down_late, down_block, down_out, mine, other,
+        turned=True,
     )
     gate = Collect(
         links, gate_in, gate_swap, gate_stage, gate_come, gate_late, gate_block, gate_out, mine, other,
@@ -1194,7 +1208,7 @@
     qkv_collect = Collect(
         links, qkv_part, qkv_swap, None, qkv_come, qkv_late, qkv_block, qkv_out, mine, other
     )
-    down.load(down_got)
+    down.load(down_got, order)
     gate.issue(order)
     small.wait()
     for m, k in ((0, 0), (1, 2)):
@@ -1213,9 +1227,9 @@
     beside.wait_recv()
     attended_back(2)
     grad_swap = send(att_grad.at[2], other_grad.at[0], bit=1)
-    for p in order:
+    first_steps = n_tensor // 2
+    for p in order[:first_steps]:
         down.step(p)
-    up.issue(order)
     for copy in loads[2:]:
         copy.wait()
     mlp_core.wait_recv()
@@ -1300,21 +1314,19 @@
 
         return send(pass_on.at[m], delta.at[2 + m], bit=1)
 
-    first_steps = n_tensor // 2
     free = -(-WINDOW // TILE)
     totals[...] = jnp.zeros_like(totals)
     grad_swap.wait_recv()
     for tile in range(free):
         back_tile(0, tile)
+    down.relay(1)
     send_halo(0)
-    down.relay(1)
-    gate.step(order[0])
+    down.step(order[first_steps])
     for tile in range(free, tiles):
         back_tile(0, tile)
-    for p in order[1:first_steps]:
-        gate.step(p)
-    for i in range(2, n_tensor - 1):
-        down.relay(i)
+    for p in order[first_steps + 1 :]:
+        down.step(p)
+    up.issue(order)
     across.wait_recv()
     both = send(g_all.at[1], g_all.at[3], bit=1)
     to_across[...] = (to_core[1].astype(f32) + from_core[1].astype(f32)).astype(bf16)
@@ -1324,6 +1336,7 @@
     both.wait_recv()
     attended_back(3)
     grad_swap = send(att_grad.at[3], other_grad.at[1], bit=1)
+    gate.step(order[0])
 
     def weight_grad(left, right, at):
         total = None
@@ -1339,19 +1352,23 @@
     links.sent.remove(both)
     out_part[...] = out_grad.reshape(n_tensor, out_quarter, width)
     grad_swap.wait_recv()
+    gate.step(order[1])
     back_tile(1, 0)
-    down.finish()
+    for i in range(2, n_tensor - 1):
+        down.relay(i)
     for tile in range(1, free):
         back_tile(1, tile)
     send_halo(1)
-    for p in order[first_steps:]:
-        gate.step(p)
     for tile in range(free, tiles):
         back_tile(1, tile)
+    for p in order[2 : n_tensor - 1]:
+        gate.step(p)
     swap0 = finish_block(0)
     gate.relay(1)
-    up.step(order[0])
     swap1 = finish_block(1)
+    down.finish()
+    for p in order[n_tensor - 1 :]:
+        gate.step(p)
 
     def project_back(b):
         units = qkv.shape[0] * quarter
@@ -1378,8 +1395,7 @@
     hidden[...] = project_back(0)
     core_send0.wait_recv()
     hidden[...] += from_core[0].astype(f32)
-    for p in order[1 : n_tensor - 1]:
-        up.step(p)
+    up.step(order[0])
     attn_row = None
     for p in range(n_tensor):
         at = slice(p * quarter, (p + 1) * quarter)
@@ -1399,10 +1415,7 @@
         move(hidden_grad.at[:, pl.ds(0, half)], totals.at[0, pl.ds(0, rows)]),
         move(hidden_grad.at[:, pl.ds(half, half)], totals.at[1, pl.ds(0, rows)]),
     ]
-    for p in order[n_tensor - 1 :]:
-        up.step(p)
-    for i in range(2, n_tensor - 1):
-        gate.relay(i)
+    up.step(order[1])
     gain = jnp.concatenate([gains[i, 2:3, : width // n_dp] for i in range(n_dp)], axis=1)
     for copy in finals:
         copy.wait()
@@ -1417,22 +1430,33 @@
         change = inverse * scaled - features * (inverse * inverse * inverse) * mean
         n1_all[1, at, :half] = (totals[0, at, :] + change[:, :half]).astype(bf16)
         n1_all[1, at, half:] = (totals[1, at, :] + change[:, half:]).astype(bf16)
+        if i == 0:
+            for j in range(2, n_tensor - 1):
+                gate.relay(j)
         if i == 1:
-            up.relay(1)
+            for p in order[2 : n_tensor - 1]:
+                up.step(p)
     save(n1_all.at[1], input_out)
     gate.finish()
-    for p in order[: n_tensor - 1]:
+    for p in order[n_tensor - 1 :]:
+        up.step(p)
+    up.relay(1)
+    for p in order[:2]:
         qkv_collect.step(p)
     for i in range(2, n_tensor - 1):
         up.relay(i)
+    for p in order[2 : n_tensor - 1]:
+        qkv_collect.step(p)
+    up.finish()
     for p in order[n_tensor - 1 :]:
         qkv_collect.step(p)
     qkv_collect.relay(1)
-    up.finish()
-    for p in order:
+    for p in order[:2]:
         out_collect.step(p)
     for i in range(2, n_tensor - 1):
         qkv_collect.relay(i)
+    for p in order[2:]:
+        out_collect.step(p)
     out_collect.relay(1)
     qkv_collect.finish()
     for i in range(2, n_tensor - 1):
@@ -1470,7 +1494,7 @@
     outs = [
         shape((rows, width)), shape((rows, width)), finals(4), shape((GROUP * quarters[3], chunk)),
         shape((chunk, GROUP * quarters[1])), shape((chunk, GROUP * quarters[2])),
-        shape((GROUP * quarters[0], chunk)),
+        shape((chunk, GROUP * quarters[0])),
     ]
     full = (GROUP, rows, width)
     scratch = [
@@ -1508,7 +1532,7 @@
     scratch += [pltpu.VMEM((q, half), bf16) for q in quarters]
     scratch += [
         pltpu.VMEM((GROUP, chunk, q) if turned else (GROUP, q, chunk), bf16)
-        for q, turned in zip(quarters, (False, True, True, False, False))
+        for q, turned in zip(quarters, (True, True, True, False, False))
     ]
     scratch += [
         pltpu.SemaphoreType.DMA((160,)),
@@ -1580,7 +1604,7 @@
         gains[1],
         gate_grad.astype(f32),
         up_grad.astype(f32),
-        down_grad.astype(f32),
+        down_grad.T.astype(f32),
     )
 
 

time: 417 us -> 401 us (0.962)
  Pallas kernels: 396 us -> 384 us
  local copies, waits for them, and re-layouts: 12 us -> 7.22 us
    pallas_call x1, Pallas kernels: 80 us -> 70.8 us  [feed(): pl.pallas_call(functools.partial(kernel_feed, n_dp, n_tensor), in_specs=[...]
    pallas_call x1, Pallas kernels: 165 us -> 160 us  [forward(): pl.pallas_call(functools.partial(kernel_forward, n_dp, n_tensor), in_spec...]
    unnamed x16 -> x13, local copies, waits for them, and re-layouts: 8.59 us -> 3.81 us
where the time goes in v1:
time: 401 us; the launch traced here: 398 us
  Pallas kernels  384 us (96%)
  local copies, waits for them, and re-layouts  7.22 us (2%)
  other arithmetic  5.61 us (1%)
    pallas_call x1, Pallas kernels, forward(): pl.pallas_call(functools.partial(kernel_forward, n_dp, n_tensor), in_spec...  160 us
    pallas_call x1, Pallas kernels, backward(): pl.pallas_call(functools.partial(kernel_backward, n_dp, n_tensor), in_spe...  154 us
    pallas_call x1, Pallas kernels, feed(): pl.pallas_call(functools.partial(kernel_feed, n_dp, n_tensor), in_specs=[...  70.8 us

profile of v1, /device:TPU:0, one launch (start us, length us, event | category | flops | bytes accessed | tf_op | source)
XLA Modules:
  0.0 398.2 jit_solution(5795283711477566352)
XLA Ops:
  0.6 0.7 stack.9
  1.3 0.7 stack.10
  2.0 0.6 pad_maximum_fusion.gain_rows
  2.5 159.6 %forward.1 = (bf16[4,384,1536]{2,1,0:T(8,128)(2,1)}, bf16[4,384,1536]{2,1,0:T(8,128)(2,1)}, f32[384,1536]{1,0:T(8,128)}, bf16[2,384,768]{2,1,0:T(8,128)(2,1)}, b...) custom-call(bf16[384,1536]{1,0:T(8,128)(2,1)} %tokens.3, ...), custom_call_target="tpu_custom_call" | custom-call | tf_op jit(solution)/shard_map/forward/pallas_call | solution.py:809
  162.1 70.8 %feed.1 = (f32[384,1536]{1,0:T(8,128)}, bf16[384,1536]{1,0:T(8,128)(2,1)}, bf16[4,384,1536]{2,1,0:T(8,128)(2,1)}, bf16[4,256,1536]{2,1,0:T(8,128)(2,1)}, bf16[4,...) custom-call(bf16[4,384,1536]{2,1,0:T(8,128)(2,1)} %get-tuple-element.4, ...), custom_call_target="tpu_custom_call" | custom-call | tf_op jit(solution)/shard_map/feed/pallas_call | solution.py:1001
  232.9 154.0 %backward.1 = (bf16[384,1536]{1,0:T(8,128)(2,1)}, bf16[384,1536]{1,0:T(8,128)(2,1)}, bf16[4,208,192]{2,1,0:T(8,128)(2,1)}, bf16[384,192]{1,0:T(8,128)(2,1)}, bf1...) custom-call(bf16[384,1536]{1,0:T(8,128)(2,1)} %get-tuple-element.47.grad_own, ...), custom_call_target="tpu_custom_call" | custom-call | tf_op jit(solution)/shard_map/backward/pallas_call | solution.py:1542
  387.0 0.0 copy-start.4
  387.0 0.8 convert_reduce_fusion
  387.8 1.0 slice.10
  388.8 1.2 convert_divide_fusion
  390.1 1.8 copy.21
  391.8 0.0 copy-start.3
  391.8 0.1 bitcast_convert_fusion
  391.9 0.0 copy-start.2
  391.9 1.1 copy.20
  393.0 0.0 copy-start.1
  393.0 0.0 copy-done.4
  393.0 1.0 convert_element_type.46
  394.0 0.0 copy-done.3
  394.0 1.0 convert_element_type.47
  394.9 0.0 copy-done.2
  394.9 0.0 copy-start
  395.0 1.0 convert_bitcast_fusion
  395.9 0.0 copy-done.1
  395.9 1.0 copy.24
  396.9 0.0 copy-done
  396.9 1.0 copy.25
Async XLA Ops:
  387.0 6.0 %copy-start.4 = (bf16[192,1024]{1,0:T(8,128)(2,1)S(1)}, bf16[192,1024]{1,0:T(8,128)(2,1)}, u32[]{:S(2)}) copy-start(bf16[192,1024]{1,0:T(8,128)(2,1)} %get-tuple-element.68) | copy-start | bytes 1179652
  391.8 2.1 copy-start.3
  391.9 3.0 copy-start.2
  393.0 2.9 copy-start.1
  394.9 2.0 copy-start
